TPU v7x, 32 devices: a whole 2x2x4 slice. The times are simulated.
32 devices in a mesh: seq: 4 (over z), shard: 8 (over y, x, core).
Axes of the slice: x: 2, y: 2, z: 4, core: 2. Of those that a mesh axis runs over, the one named last changes fastest.
Arguments:
- tokens: bfloat16 [8, 2048, 1024], P('shard', 'seq'), may hold values from -6 to 6
- ln1_gain: bfloat16 [1024], P(('seq', 'shard')), may hold values from 0.5 to 1.5
- ln1_bias: bfloat16 [1024], P(('seq', 'shard')), may hold values from -3 to 3
- w_qkv: bfloat16 [1024, 3072], P(('seq', 'shard')), may hold values from -0.1875 to 0.1875
- bias_query: bfloat16 [1024], P(('seq', 'shard')), may hold values from -3 to 3
- bias_value: bfloat16 [1024], P(('seq', 'shard')), may hold values from -3 to 3
- w_out: bfloat16 [1024, 1024], P(('seq', 'shard')), may hold values from -1 to 1
- bias_out: bfloat16 [1024], P(('seq', 'shard')), may hold values from -3 to 3
- ln2_gain: bfloat16 [1024], P(('seq', 'shard')), may hold values from 0.5 to 1.5
- ln2_bias: bfloat16 [1024], P(('seq', 'shard')), may hold values from -3 to 3
- w_in: bfloat16 [1024, 4096], P(('seq', 'shard')), may hold values from -0.1875 to 0.1875
- bias_in: bfloat16 [4096], P(('seq', 'shard')), may hold values from -3 to 3
- w_back: bfloat16 [4096, 1024], P(('seq', 'shard')), may hold values from -0.09375 to 0.09375
- bias_back: bfloat16 [1024], P(('seq', 'shard')), may hold values from -3 to 3
- cotangent: bfloat16 [8, 2048, 1024], P('shard', 'seq'), may hold values from -6 to 6
Outputs:
- result: bfloat16 [8, 2048, 1024], P('shard', 'seq')
- grad_tokens: float32 [8, 2048, 1024], P('shard', 'seq')
- grad_ln1_gain: float32 [1024], P(('seq', 'shard'))
- grad_ln1_bias: float32 [1024], P(('seq', 'shard'))
- grad_w_qkv: float32 [1024, 3072], P(('seq', 'shard'))
- grad_bias_query: float32 [1024], P(('seq', 'shard'))
- grad_bias_value: float32 [1024], P(('seq', 'shard'))
- grad_w_out: float32 [1024, 1024], P(('seq', 'shard'))
- grad_bias_out: float32 [1024], P(('seq', 'shard'))
- grad_ln2_gain: float32 [1024], P(('seq', 'shard'))
- grad_ln2_bias: float32 [1024], P(('seq', 'shard'))
- grad_w_in: float32 [1024, 4096], P(('seq', 'shard'))
- grad_bias_in: float32 [4096], P(('seq', 'shard'))
- grad_w_back: float32 [4096, 1024], P(('seq', 'shard'))
- grad_bias_back: float32 [1024], P(('seq', 'shard'))
All inputs are finite; a program needn't handle non-finite values.
Results may differ from a plain program's by a relative error of at most 0.014.
The roundings to bfloat16 on the way count: a program that leaves them out, or rounds other values in their place, can miss the bound.
Values may be sent and summed in bfloat16 or wider, within the bound.
A program may use at most 192 MiB of HBM per device.

v0:
```python
import math
import jax
import jax.numpy as jnp
from jax import lax
from jax.sharding import PartitionSpec as P

HEAD_DIM = 64
norm_eps = 1e-05
gelu_c = math.sqrt(2.0 / math.pi)


def normalize(values):
    mean_row = jnp.mean(values, axis=-1, keepdims=True)
    centred = values - mean_row
    var_row = jnp.mean(centred * centred, axis=-1, keepdims=True)
    scale_row = lax.rsqrt(var_row + norm_eps)
    return (centred * scale_row, scale_row)


def norm_back(dnormed, normed, scale_row):
    return scale_row * (
        dnormed
        - jnp.mean(dnormed, axis=-1, keepdims=True)
        - normed * jnp.mean(dnormed * normed, axis=-1, keepdims=True)
    )


def gelu_pair(inputs):
    inner = gelu_c * (inputs + 0.044715 * inputs * inputs * inputs)
    tanh_val = jnp.tanh(inner)
    value = 0.5 * inputs * (1.0 + tanh_val)
    slope = 0.5 * (1.0 + tanh_val) + 0.5 * inputs * (1.0 - tanh_val * tanh_val) * gelu_c * (
        1.0 + 3.0 * 0.044715 * inputs * inputs
    )
    return (value, slope)


def masked_scores(query_block, keys, start, scale):
    block = query_block.shape[0]
    length = keys.shape[0]
    scores = (
        jnp.einsum("qgd,kgd->gqk", query_block, keys, preferred_element_type=jnp.float32) * scale
    )
    q_pos = start + jnp.arange(block, dtype=jnp.int32)
    k_pos = jnp.arange(length, dtype=jnp.int32)
    allowed = k_pos[None, None, :] <= q_pos[None, :, None]
    return jnp.where(allowed, scores, -1e30)


def attend_forward(query, keys, values):
    length, groups, width = query.shape
    block = min(512, length)
    scale = 1.0 / math.sqrt(width)

    def one_block(index):
        start = index * block
        q_blk = lax.dynamic_slice_in_dim(query, start, block, 0)
        scores = masked_scores(q_blk, keys, start, scale)
        log_total = jnp.log(jnp.sum(jnp.exp(scores), axis=-1))
        probs = jnp.exp(scores - log_total[:, :, None]).astype(jnp.bfloat16)
        attended = jnp.einsum("gqk,kgd->qgd", probs, values, preferred_element_type=jnp.float32)
        return (attended.astype(jnp.bfloat16), log_total)

    outs, logs = lax.map(one_block, jnp.arange(length // block, dtype=jnp.int32))
    return (outs.reshape(length, groups, width), logs)


def attend_backward(query, keys, values, attended, logs, d_att):
    length, groups, width = query.shape
    block = min(512, length)
    scale = 1.0 / math.sqrt(width)

    def one_block(carry, index):
        d_keys, d_values = carry
        start = index * block
        q_blk = lax.dynamic_slice_in_dim(query, start, block, 0)
        o_blk = lax.dynamic_slice_in_dim(attended, start, block, 0)
        do_blk = lax.dynamic_slice_in_dim(d_att, start, block, 0)
        scores = masked_scores(q_blk, keys, start, scale)
        log_total = lax.dynamic_index_in_dim(logs, index, 0, keepdims=False)
        probs = jnp.exp(scores - log_total[:, :, None])
        probs_b = probs.astype(jnp.bfloat16)
        d_values = d_values + jnp.einsum(
            "gqk,qgd->kgd", probs_b, do_blk, preferred_element_type=jnp.float32
        )
        d_probs = jnp.einsum("qgd,kgd->gqk", do_blk, values, preferred_element_type=jnp.float32)
        delta = jnp.swapaxes(
            jnp.sum(do_blk.astype(jnp.float32) * o_blk.astype(jnp.float32), axis=-1), 0, 1
        )
        d_scores = (probs * (d_probs - delta[:, :, None]) * scale).astype(jnp.bfloat16)
        d_query = jnp.einsum(
            "gqk,kgd->qgd", d_scores, keys, preferred_element_type=jnp.float32
        ).astype(jnp.bfloat16)
        d_keys = d_keys + jnp.einsum(
            "gqk,qgd->kgd", d_scores, q_blk, preferred_element_type=jnp.float32
        )
        return ((d_keys, d_values), d_query)

    zeros = jnp.zeros((length, groups, width), jnp.float32)
    (d_keys, d_values), d_queries = lax.scan(
        one_block, (zeros, zeros), jnp.arange(length // block, dtype=jnp.int32)
    )
    return (
        d_queries.reshape(length, groups, width),
        d_keys.astype(jnp.bfloat16),
        d_values.astype(jnp.bfloat16),
    )


def col_dot(left, right):
    return lax.dot_general(
        left, right, (((0,), (0,)), ((), ())), preferred_element_type=jnp.float32
    )


def row_dot(left, right):
    return lax.dot_general(
        left, right, (((1,), (1,)), ((), ())), preferred_element_type=jnp.float32
    )


def per_device(
    tokens,
    ln1_gain,
    ln1_bias,
    w_qkv,
    bias_query,
    bias_value,
    w_out,
    bias_out,
    ln2_gain,
    ln2_bias,
    w_in,
    bias_in,
    w_back,
    bias_back,
    cotangent,
):
    f32 = jnp.float32
    params = (
        lax.all_gather(ln1_gain, ("seq", "shard"), axis=0, tiled=True),
        lax.all_gather(ln1_bias, ("seq", "shard"), axis=0, tiled=True),
        lax.all_gather(w_qkv, ("seq", "shard"), axis=0, tiled=True),
        lax.all_gather(bias_query, ("seq", "shard"), axis=0, tiled=True),
        lax.all_gather(bias_value, ("seq", "shard"), axis=0, tiled=True),
        lax.all_gather(w_out, ("seq", "shard"), axis=0, tiled=True),
        lax.all_gather(bias_out, ("seq", "shard"), axis=0, tiled=True),
        lax.all_gather(ln2_gain, ("seq", "shard"), axis=0, tiled=True),
        lax.all_gather(ln2_bias, ("seq", "shard"), axis=0, tiled=True),
        lax.all_gather(w_in, ("seq", "shard"), axis=0, tiled=True),
        lax.all_gather(bias_in, ("seq", "shard"), axis=0, tiled=True),
        lax.all_gather(w_back, ("seq", "shard"), axis=0, tiled=True),
        lax.all_gather(bias_back, ("seq", "shard"), axis=0, tiled=True),
    )
    (
        g_one,
        s_one,
        full_qkv,
        full_bq,
        full_bv,
        full_out,
        full_bo,
        g_two,
        s_two,
        full_in,
        full_bin,
        full_back,
        full_bback,
    ) = params
    rows = tokens.shape[1]
    width = tokens.shape[2]
    x_f = tokens[0].astype(f32)
    normed1, scale1 = normalize(x_f)
    h_one = (normed1 * g_one.astype(f32) + s_one.astype(f32)).astype(jnp.bfloat16)
    bias_qkv = jnp.concatenate([full_bq.astype(f32), jnp.zeros((width,), f32), full_bv.astype(f32)])
    qkv = (jnp.dot(h_one, full_qkv, preferred_element_type=f32) + bias_qkv).astype(jnp.bfloat16)
    grouped = lax.all_to_all(
        qkv.reshape(rows, 3, width), "seq", split_axis=2, concat_axis=0, tiled=True
    )
    length = grouped.shape[0]
    local_width = grouped.shape[2]
    groups = local_width // HEAD_DIM
    query = grouped[:, 0].reshape(length, groups, HEAD_DIM)
    keys = grouped[:, 1].reshape(length, groups, HEAD_DIM)
    values = grouped[:, 2].reshape(length, groups, HEAD_DIM)
    attended, logs = attend_forward(query, keys, values)
    att_tok = lax.all_to_all(
        attended.reshape(length, local_width), "seq", split_axis=0, concat_axis=1, tiled=True
    )
    resid = x_f + jnp.dot(att_tok, full_out, preferred_element_type=f32) + full_bo.astype(f32)
    normed2, scale2 = normalize(resid)
    h_two = (normed2 * g_two.astype(f32) + s_two.astype(f32)).astype(jnp.bfloat16)
    pre = jnp.dot(h_two, full_in, preferred_element_type=f32) + full_bin.astype(f32)
    act_val, slope = gelu_pair(pre)
    act = act_val.astype(jnp.bfloat16)
    result = (
        resid + jnp.dot(act, full_back, preferred_element_type=f32) + full_bback.astype(f32)
    ).astype(jnp.bfloat16)
    cot_b = cotangent[0]
    cot_f = cot_b.astype(f32)
    g_w_back = col_dot(act, cot_b)
    g_b_back = jnp.sum(cot_f, axis=0)
    d_pre = (row_dot(cot_b, full_back) * slope).astype(jnp.bfloat16)
    g_w_in = col_dot(h_two, d_pre)
    g_b_in = jnp.sum(d_pre.astype(f32), axis=0)
    d_h2 = row_dot(d_pre, full_in)
    g_g2 = jnp.sum(d_h2 * normed2, axis=0)
    g_s2 = jnp.sum(d_h2, axis=0)
    d_resid = cot_f + norm_back(d_h2 * g_two.astype(f32), normed2, scale2)
    d_resid_b = d_resid.astype(jnp.bfloat16)
    g_w_out = col_dot(att_tok, d_resid_b)
    g_b_out = jnp.sum(d_resid, axis=0)
    d_att_tok = row_dot(d_resid_b, full_out).astype(jnp.bfloat16)
    d_att = lax.all_to_all(d_att_tok, "seq", split_axis=1, concat_axis=0, tiled=True).reshape(
        length, groups, HEAD_DIM
    )
    d_query, d_keys, d_values = attend_backward(query, keys, values, attended, logs, d_att)
    stacked = jnp.stack(
        [
            d_query.reshape(length, local_width),
            d_keys.reshape(length, local_width),
            d_values.reshape(length, local_width),
        ],
        axis=1,
    )
    d_qkv = lax.all_to_all(stacked, "seq", split_axis=0, concat_axis=2, tiled=True).reshape(
        rows, 3 * width
    )
    g_w_qkv = col_dot(h_one, d_qkv)
    g_bq = jnp.sum(d_qkv[:, :width].astype(f32), axis=0)
    g_bv = jnp.sum(d_qkv[:, 2 * width :].astype(f32), axis=0)
    d_h1 = row_dot(d_qkv, full_qkv)
    g_g1 = jnp.sum(d_h1 * normed1, axis=0)
    g_s1 = jnp.sum(d_h1, axis=0)
    d_tokens = d_resid + norm_back(d_h1 * g_one.astype(f32), normed1, scale1)
    summed = (
        lax.psum_scatter(g_g1, ("seq", "shard"), scatter_dimension=0, tiled=True),
        lax.psum_scatter(g_s1, ("seq", "shard"), scatter_dimension=0, tiled=True),
        lax.psum_scatter(g_w_qkv, ("seq", "shard"), scatter_dimension=0, tiled=True),
        lax.psum_scatter(g_bq, ("seq", "shard"), scatter_dimension=0, tiled=True),
        lax.psum_scatter(g_bv, ("seq", "shard"), scatter_dimension=0, tiled=True),
        lax.psum_scatter(g_w_out, ("seq", "shard"), scatter_dimension=0, tiled=True),
        lax.psum_scatter(g_b_out, ("seq", "shard"), scatter_dimension=0, tiled=True),
        lax.psum_scatter(g_g2, ("seq", "shard"), scatter_dimension=0, tiled=True),
        lax.psum_scatter(g_s2, ("seq", "shard"), scatter_dimension=0, tiled=True),
        lax.psum_scatter(g_w_in, ("seq", "shard"), scatter_dimension=0, tiled=True),
        lax.psum_scatter(g_b_in, ("seq", "shard"), scatter_dimension=0, tiled=True),
        lax.psum_scatter(g_w_back, ("seq", "shard"), scatter_dimension=0, tiled=True),
        lax.psum_scatter(g_b_back, ("seq", "shard"), scatter_dimension=0, tiled=True),
    )
    (
        r_g1,
        r_s1,
        r_w_qkv,
        r_bq,
        r_bv,
        r_w_out,
        r_b_out,
        r_g2,
        r_s2,
        r_w_in,
        r_b_in,
        r_w_back,
        r_b_back,
    ) = summed
    return (
        result[None],
        d_tokens[None],
        r_g1,
        r_s1,
        r_w_qkv,
        r_bq,
        r_bv,
        r_w_out,
        r_b_out,
        r_g2,
        r_s2,
        r_w_in,
        r_b_in,
        r_w_back,
        r_b_back,
    )


def solution(mesh):
    return jax.shard_map(
        per_device,
        mesh=mesh,
        in_specs=(
            P("shard", "seq", None),
            P(("seq", "shard")),
            P(("seq", "shard")),
            P(("seq", "shard"), None),
            P(("seq", "shard")),
            P(("seq", "shard")),
            P(("seq", "shard"), None),
            P(("seq", "shard")),
            P(("seq", "shard")),
            P(("seq", "shard")),
            P(("seq", "shard"), None),
            P(("seq", "shard")),
            P(("seq", "shard"), None),
            P(("seq", "shard")),
            P("shard", "seq", None),
        ),
        out_specs=(
            P("shard", "seq", None),
            P("shard", "seq", None),
            P(("seq", "shard")),
            P(("seq", "shard")),
            P(("seq", "shard"), None),
            P(("seq", "shard")),
            P(("seq", "shard")),
            P(("seq", "shard"), None),
            P(("seq", "shard")),
            P(("seq", "shard")),
            P(("seq", "shard")),
            P(("seq", "shard"), None),
            P(("seq", "shard")),
            P(("seq", "shard"), None),
            P(("seq", "shard")),
        ),
        check_vma=False,
    )
```

profile of v0, /device:TPU:13, one launch (start us, length us, event | category | flops | bytes accessed | tf_op | source)
XLA Modules:
  0.0 1236.6 jit_solution(11690931587588916261)
XLA Ops:
  16.1 40.8 %all-reduce.18 = (bf16[1024]{0:T(1024)(128)(2,1)S(1)}, bf16[1024]{0:T(1024)(128)(2,1)S(1)}, bf16[1024]{0:T(1024)(128)(2,1)S(1)}, bf16[1024]{0:T(1024)(128)(2,1)S...) all-reduce(bf16[1024]{0:T(1024)(128)(2,1)S(1)} %dynamic-update-slic, ...), channel_id=1, replica_groups=mesh['seq'=4,'shard'=8] {'seq','shard'}, use_global_device_ids=true, to_apply=%add.3 | all-reduce | flops 8192 | bytes 32768
  60.1 21.6 %all-gather.6.cloned.1.call-done = bf16[1024,3072]{1,0:T(8,128)(2,1)} async-done(((bf16[32,3072]{1,0:T(8,128)(2,1)}), bf16[1024,3072]{1,0:T(8,128)(2,1)}) %all-gather.6.cloned.1.call-update) | async-done | bytes 6291472 | tf_op jit(solution)/shard_map/all_gather | solution.py:143
  81.7 8.4 add_convert_fusion
  90.1 3.2 copy.71
  93.3 4.6 copy.72
  97.9 5.0 all-to-all-start
  103.5 101.0 %all-to-all-done = bf16[512,3,1024]{0,1,2:T(4,128)(2,1)} async-done(((bf16[512,3,1024]{0,1,2:T(4,128)(2,1)}), bf16[512,3,1024]{0,1,2:T(4,128)(2,1)}, u32[]{:S(2)}, u32[]{:S(2)}) %all-to-all-start) | async-done | bytes 3145760 | tf_op jit(solution)/shard_map/all_to_all | solution.py:177
  204.5 3.0 copy.73
  207.5 2.9 copy.74
  216.3 50.8 %while.27 = (s32[]{:T(128)}, bf16[4,512,4,64]{1,3,2,0:T(8,128)(2,1)}, f32[4,4,512]{2,1,0:T(4,128)}, s32[4]{0:T(128)S(1)}, bf16[2048,4,64]{0,2,1:T(8,128)(2,1)S(1...) while((s32[]{:T(128)}, ...), condition=%wide.region_4.5_spmd, body=%wide.region_2.4_spmd.sunk | while | flops 1104280064 | bytes 43569372 | solution.py:64
  218.2 4.7 exponential_reduce_fusion.2
  222.9 5.5 fusion.127
  230.9 4.7 exponential_reduce_fusion.2
  235.6 5.5 fusion.127
  243.6 4.7 exponential_reduce_fusion.2
  248.3 5.5 fusion.127
  256.3 4.7 exponential_reduce_fusion.2
  261.0 5.5 fusion.127
  268.1 7.5 all-to-all-start.1
  275.6 54.4 %all-gather = bf16[32,1,128]{2,1,0:T(2,128)(2,1)S(1)} all-gather(bf16[1,1,128]{2,1,0:T(2,128)(2,1)S(1)} %bitcast.188), channel_id=1, replica_groups=mesh['seq'=4,'shard'=8] {'seq','shard'}, dimensions={0}, use_global_device_ids=true | all-gather | bytes 8448 | tf_op jit(solution)/shard_map/all_gather | solution.py:151
  331.1 3.6 fusion.86
  335.1 10.6 fusion.83
  345.7 11.9 all-gather.12.cloned.1.call-done
  357.6 14.9 %convert_reduce_fusion = (f32[4096]{0:T(1024)}, bf16[512,4096]{1,0:T(8,128)(2,1)}) fusion(f32[512,4096]{1,0:T(8,128)} %fusion.83, f32[4096]{0:T(1024)S(1)} %bitcast.185, bf16[4096,1024]{1,0:T(8,128)(2,1)} %all-gather.12.cloned.1.call-done, bf16[1,512,1024]{2,1,0:T(8,128)(2,1)} %param.33), kind=kOutput, calls=%fused_computation.52 | convolution fusion | flops 4341100544 | bytes 22052864 | tf_op jit(solution)/shard_map/dot_general | solution.py:117
  372.5 7.7 multiply_reduce_fusion.1
  380.2 3.3 fusion.84
  385.9 4.4 all-to-all-start.2
  390.4 2.4 copy.86
  392.8 4.5 fusion.79
  397.3 15.6 %all-to-all-done.2 = bf16[512,4,256]{2,0,1:T(8,128)(2,1)} async-done(((bf16[512,4,256]{2,0,1:T(8,128)(2,1)}), bf16[512,4,256]{2,0,1:T(8,128)(2,1)}, u32[]{:S(2)}, u32[]{:S(2)}) %all-to-all-start.2) | async-done | bytes 1048608 | tf_op jit(solution)/shard_map/all_to_all | solution.py:214
  416.7 156.1 %while.28 = (s32[]{:T(128)}, f32[2048,4,64]{0,2,1:T(8,128)}, f32[2048,4,64]{0,2,1:T(8,128)}, bf16[4,512,4,64]{1,3,2,0:T(8,128)(2,1)}, s32[4]{0:T(128)S(1)}, /*in...) while((s32[]{:T(128)}, f32[2048,4,64]{0,2,1:T(8,128)}, ...), condition=%wide.region_11.12_spmd.clone, body=%wide.region_9.11_spmd.clone.sunk | while | flops 2734291456 | bytes 138236336 | solution.py:100
  422.6 3.5 fusion.138
  426.2 7.2 fusion.140
  433.4 10.5 multiply_convert_fusion.5
  443.9 7.0 fusion.141
  450.9 4.0 fusion.139
  460.7 3.5 fusion.138
  464.3 7.6 fusion.140
  471.9 10.5 multiply_convert_fusion.5
  482.4 7.0 fusion.141
  489.4 4.8 fusion.139
  499.8 3.5 fusion.138
  503.4 7.6 fusion.140
  511.0 10.5 multiply_convert_fusion.5
  521.5 6.9 fusion.141
  528.5 4.8 fusion.139
  539.0 3.5 fusion.138
  542.5 7.6 fusion.140
  550.1 10.5 multiply_convert_fusion.5
  560.6 6.9 fusion.141
  567.6 4.8 fusion.139
  578.9 4.8 copy.82
  583.7 97.2 %all_to_all.68 = bf16[2048,3,256]{2,1,0:T(4,128)(2,1)S(1)} all-to-all(bf16[2048,3,256]{2,1,0:T(4,128)(2,1)} %copy.82), channel_id=1, replica_groups=mesh['seq'=4,'shard'=8] {'seq'}, dimensions={0} | all-to-all | bytes 6291456 | tf_op jit(solution)/shard_map/all_to_all | solution.py:226
  683.0 4.8 copy.84
  687.8 8.7 fusion.65
  697.7 16.2 %fusion.68 = f32[4096,1024]{1,0:T(8,128)} fusion(bf16[1,512,1024]{2,1,0:T(8,128)(2,1)S(1)} %copy-done.16, f32[512,4096]{1,0:T(8,128)} %fusion.83, f32[4096]{0:T(1024)S(1)} %bitcast.186), kind=kOutput, calls=%fused_computation.98 | convolution fusion | flops 4315938816 | bytes 26230784 | tf_op jit(solution)/shard_map/dot_general | solution.py:111
  715.7 11.5 fusion.82
  727.8 13.2 %fusion.63 = bf16[1,512,1024]{2,1,0:T(8,128)(2,1)} fusion(f32[512,1024]{1,0:T(8,128)S(1)} %copy-done.6, bf16[4096,1024]{1,0:T(8,128)(2,1)} %all-gather.12.cloned.1.call-done, f32[1024]{0:T(1024)S(1)} %convert_element_type.124, f32[512,4096]{1,0:T(8,128)} %fusion.83, f32[4096]{0:T(1024)S(1)} %bitcast.187), kind=kOutput, calls=%fused_computation.94 | convolution fusion | flops 4317511680 | bytes 19943424 | tf_op jit(solution)/shard_map/dot_general | solution.py:197
  741.5 8.8 fusion.56
  750.3 45.6 %all-reduce.17 = (f32[1024]{0:T(1024)S(1)}, f32[1024]{0:T(1024)S(1)}, f32[1024]{0:T(1024)S(1)}, f32[1024]{0:T(1024)S(1)}, f32[1024]{0:T(1024)S(1)}, /*index=5*/f...) all-reduce(f32[1024]{0:T(1024)S(1)} %get-tuple-element.184, ...), channel_id=2, replica_groups=mesh['seq'=4,'shard'=8] {'seq','shard'}, use_global_device_ids=true, to_apply=%region_15.16.clone | all-reduce | flops 12288 | bytes 98304
  801.2 3.6 fusion.55
  804.8 48.2 %reduce-scatter.5.cloned.1.call-done = f32[32,3072]{1,0:T(8,128)} async-done(((f32[1024,3072]{1,0:T(8,128)}), f32[32,3072]{1,0:T(8,128)}) %reduce-scatter.5.cloned.1.call-update) | async-done | bytes 393232 | tf_op jit(solution)/shard_map/reduce_scatter | solution.py:239
  853.0 189.0 %reduce-scatter.11.cloned.1.call-done = f32[128,1024]{1,0:T(8,128)} async-done(((f32[4096,1024]{1,0:T(8,128)}), f32[128,1024]{1,0:T(8,128)}) %reduce-scatter.11.cloned.1.call-update) | async-done | bytes 524304 | tf_op jit(solution)/shard_map/reduce_scatter | solution.py:248
  1042.1 187.5 %reduce-scatter.9.cloned.1.call-done = f32[32,4096]{1,0:T(8,128)} async-done(((f32[1024,4096]{1,0:T(8,128)}), f32[32,4096]{1,0:T(8,128)}) %reduce-scatter.9.cloned.1.call-update) | async-done | bytes 524304 | tf_op jit(solution)/shard_map/reduce_scatter | solution.py:246
  (254 shorter events, 64.4 us)
Async XLA Ops:
  7.2 74.5 %all-gather.6.cloned.1.call-start = ((), (), s32[]{:S(2)}) async-start(), calls=%async_computation.8 | async-start | bytes 6488064 | tf_op jit(solution)/shard_map/all_gather | solution.py:143
  7.9 322.1 %all-gather.8.cloned.1.call-start = ((), (), s32[]{:S(2)}) async-start(), calls=%async_computation.9 | async-start | bytes 2162688 | tf_op jit(solution)/shard_map/all_gather | solution.py:146
  8.7 326.5 %all-gather.10.cloned.1.call-start = ((), (), s32[]{:S(2)}) async-start(), calls=%async_computation.10 | async-start | bytes 8650752 | tf_op jit(solution)/shard_map/all_gather | solution.py:150
  56.9 24.8 %copy-start.25 = (f32[1024]{0:T(1024)}, f32[1024]{0:T(1024)S(1)}, u32[]{:S(2)}) copy-start(f32[1024]{0:T(1024)S(1)} %convert_element_type.112) | copy-start | bytes 12292
  56.9 24.8 %copy-start.38 = (f32[1024]{0:T(1024)}, f32[1024]{0:T(1024)S(1)}, u32[]{:S(2)}) copy-start(f32[1024]{0:T(1024)S(1)} %convert_element_type.113) | copy-start | bytes 12292
  58.4 23.3 %copy-start.21 = (f32[512]{0:T(512)}, f32[512]{0:T(512)S(1)}, u32[]{:S(2)}) copy-start(f32[512]{0:T(512)S(1)} %broadcast_multiply_fusion.5) | copy-start | bytes 6148
  60.1 21.7 %copy-start.34 = (f32[512]{0:T(512)}, f32[512]{0:T(512)S(1)}, u32[]{:S(2)}) copy-start(f32[512]{0:T(512)S(1)} %add_rsqrt_fusion.1) | copy-start | bytes 6148
  97.9 106.6 %all-to-all-start = ((bf16[512,3,1024]{0,1,2:T(4,128)(2,1)}), bf16[512,3,1024]{0,1,2:T(4,128)(2,1)}, u32[]{:S(2)}, u32[]{:S(2)}) async-start(bf16[512,3,1024]{0,1,2:T(4,128)(2,1)} %copy.72), calls=%async_computation | async-start | bytes 8388608 | tf_op jit(solution)/shard_map/all_to_all | solution.py:177
  103.0 254.6 %all-gather.12.cloned.1.call-start = ((), (), s32[]{:S(2)}) async-start(), calls=%async_computation.11 | async-start | bytes 8650752 | tf_op jit(solution)/shard_map/all_gather | solution.py:152
  216.3 59.3 %copy-start.43 = (bf16[128]{0:T(256)(128)(2,1)S(1)}, bf16[128]{0:T(256)(128)(2,1)}, u32[]{:S(2)}) copy-start(bf16[128]{0:T(256)(128)(2,1)} %param.30) | copy-start | bytes 772
  218.2 4.7 copy-start.17
  230.9 4.7 copy-start.17
  243.6 4.7 copy-start.17
  256.3 4.7 copy-start.17
  268.1 61.9 %all-to-all-start.1 = ((bf16[4,512,256]{1,2,0:T(8,128)(2,1)}), bf16[4,512,256]{1,2,0:T(8,128)(2,1)S(1)}, u32[]{:S(2)}, u32[]{:S(2)}) async-start(bf16[4,512,256]{1,2,0:T(8,128)(2,1)} %bitcast.12), calls=%async_computation.1 | async-start | bytes 2097152 | tf_op jit(solution)/shard_map/all_to_all | solution.py:187
  275.6 104.6 %copy-start.27 = (f32[1024]{0:T(1024)}, f32[1024]{0:T(1024)S(1)}, u32[]{:S(2)}) copy-start(f32[1024]{0:T(1024)S(1)} %convert_element_type.119) | copy-start | bytes 12292
  275.6 59.6 %copy-start.40 = (f32[1024]{0:T(1024)}, f32[1024]{0:T(1024)S(1)}, u32[]{:S(2)}) copy-start(f32[1024]{0:T(1024)S(1)} %convert_element_type.120) | copy-start | bytes 12292
  330.0 27.6 %copy-start.30 = (f32[32,1,128]{2,1,0:T(1,128)}, f32[32,1,128]{2,1,0:T(1,128)S(1)}, u32[]{:S(2)}) copy-start(f32[32,1,128]{2,1,0:T(1,128)S(1)} %convert_element_type.137) | copy-start | bytes 49156
  334.7 37.8 %copy-start.5 = (f32[512,1024]{1,0:T(8,128)}, f32[512,1024]{1,0:T(8,128)S(1)}, u32[]{:S(2)}) copy-start(f32[512,1024]{1,0:T(8,128)S(1)} %get-tuple-element.254) | copy-start | bytes 6291460
  334.7 45.5 %copy-start.19 = (f32[512]{0:T(512)}, f32[512]{0:T(512)S(1)}, u32[]{:S(2)}) copy-start(f32[512]{0:T(512)S(1)} %broadcast_multiply_fusion.4) | copy-start | bytes 6148
  335.1 45.1 %copy-start.32 = (f32[512]{0:T(512)}, f32[512]{0:T(512)S(1)}, u32[]{:S(2)}) copy-start(f32[512]{0:T(512)S(1)} %add_rsqrt_fusion) | copy-start | bytes 6148
  357.6 14.9 %copy-start.44 = (bf16[1024,4096]{1,0:T(8,128)(2,1)S(1)}, bf16[1024,4096]{1,0:T(8,128)(2,1)}, u32[]{:S(2)}) copy-start(bf16[1024,4096]{1,0:T(8,128)(2,1)} %all-gather.10.cloned.1.call-done) | copy-start | bytes 25165828
  372.5 7.7 copy-start.15
  380.2 3.4 copy-start.14
  383.6 9.2 copy-start.3
  385.9 27.0 %all-to-all-start.2 = ((bf16[512,4,256]{2,0,1:T(8,128)(2,1)}), bf16[512,4,256]{2,0,1:T(8,128)(2,1)}, u32[]{:S(2)}, u32[]{:S(2)}) async-start(bf16[512,4,256]{2,0,1:T(8,128)(2,1)} %bitcast.179), calls=%async_computation.2 | async-start | bytes 2097152 | tf_op jit(solution)/shard_map/all_to_all | solution.py:214
  390.4 414.4 %reduce-scatter.7.cloned.1.call-start = ((), (), s32[]{:S(2)}) async-start(), calls=%async_computation.13 | async-start | bytes 4325376 | tf_op jit(solution)/shard_map/reduce_scatter | solution.py:242
  397.2 455.8 %reduce-scatter.5.cloned.1.call-start = ((), (), s32[]{:S(2)}) async-start(), calls=%async_computation.12 | async-start | bytes 12976128 | tf_op jit(solution)/shard_map/reduce_scatter | solution.py:239
  416.9 5.1 copy-start.11
  420.9 5.3 copy-start.18
  422.6 3.6 copy-start.2
  443.9 7.0 copy-start
  450.9 4.0 copy-start.12
  455.0 5.0 copy-start.11
  459.0 5.3 copy-start.18
  460.7 3.6 copy-start.2
  482.4 7.0 copy-start
  489.4 4.8 copy-start.12
  494.1 5.0 copy-start.11
  498.1 5.3 copy-start.18
  499.8 3.6 copy-start.2
  521.5 6.9 copy-start
  528.5 4.8 copy-start.12
  533.2 5.0 copy-start.11
  537.2 5.3 copy-start.18
  538.9 3.6 copy-start.2
  560.6 6.9 copy-start
  567.6 4.8 copy-start.12
  572.8 3.8 copy-start.1
  576.6 2.0 copy-start.13
  682.9 4.8 copy-start.7
  682.9 4.8 copy-start.22
  682.9 4.8 copy-start.26
  682.9 4.8 copy-start.35
  683.0 4.8 copy-start.39
  696.5 345.6 %reduce-scatter.11.cloned.1.call-start = ((), (), s32[]{:S(2)}) async-start(), calls=%async_computation.15 | async-start | bytes 17301504 | tf_op jit(solution)/shard_map/reduce_scatter | solution.py:248
  714.0 515.6 %reduce-scatter.9.cloned.1.call-start = ((), (), s32[]{:S(2)}) async-start(), calls=%async_computation.14 | async-start | bytes 17301504 | tf_op jit(solution)/shard_map/reduce_scatter | solution.py:246
  727.8 13.2 %copy-start.10 = (bf16[512,3,4,256]{0,3,2,1:T(8,128)(2,1)S(1)}, bf16[512,3,4,256]{0,3,2,1:T(8,128)(2,1)}, u32[]{:S(2)}) copy-start(bf16[512,3,4,256]{0,3,2,1:T(8,128)(2,1)} %copy.84) | copy-start | bytes 9437188
  741.4 8.8 copy-start.23
  741.4 8.8 copy-start.24
  741.4 8.8 copy-start.29
  741.4 8.8 copy-start.36
  741.4 8.8 copy-start.37
  741.5 59.7 %copy-start.4 = (f32[512,1024]{1,0:T(8,128)S(1)}, f32[512,1024]{1,0:T(8,128)}, u32[]{:S(2)}) copy-start(f32[512,1024]{1,0:T(8,128)} %copy-done.3) | copy-start | bytes 6291460
  (10 other events, 13.9 us)
Sparse Core Ops, SparseCore 0:
  10.8 70.8 all-gather.5
  84.6 102.7 all-gather.7
  190.2 78.1 all-gather.9
  271.1 86.4 all-gather.11
  397.4 115.2 reduce-scatter.6
  696.6 156.3 reduce-scatter.4
  855.9 186.1 reduce-scatter.10
  1044.9 184.6 reduce-scatter.8
where the time goes:
time: 1250 us; the launch traced here: 1240 us
  waiting for transfers between devices  577 us (46%)
  matrix products  282 us (23%)
  blocking collectives  238 us (19%)
  local copies, waits for them, and re-layouts  70.1 us (6%)
  other arithmetic  22.6 us (2%)
  starting transfers between devices  17.6 us (1%)
  between operations  14.8 us (1%)
  loops' own time  14 us (1%)
    reduce_scatter x1, waiting for transfers between devices, per_device(): lax.psum_scatter(g_w_back, ('seq', 'shard'), scatter_dimension=0, tiled=T...  189 us
    reduce_scatter x1, waiting for transfers between devices, per_device(): lax.psum_scatter(g_w_in, ('seq', 'shard'), scatter_dimension=0, tiled=True)  188 us
    all_to_all x1, waiting for transfers between devices, per_device(): lax.all_to_all(qkv.reshape(rows, 3, width), 'seq', split_axis=2, concat_a...  101 us
    all_to_all x1, blocking collectives, per_device(): lax.all_to_all(stacked, 'seq', split_axis=0, concat_axis=2, tiled=True)  97.2 us
    unnamed x2, blocking collectives  86.4 us
    all_gather x1, blocking collectives, per_device(): lax.all_gather(bias_in, ('seq', 'shard'), axis=0, tiled=True)  54.4 us
    reduce_scatter x1, waiting for transfers between devices, per_device(): lax.psum_scatter(g_w_qkv, ('seq', 'shard'), scatter_dimension=0, tiled=True)  48.2 us
    dot_general x4, matrix products, one_block(): jnp.einsum('qgd,kgd->gqk', do_blk, values, preferred_element_type=jnp.flo...  42 us
  transfers between devices with their start and end apart: 11, of which 7 were waited for; matrix products, arithmetic and copies ran while one was open for 28% of the time, Pallas kernels for 0%

commit v1 on v0

--- a/solution.py
+++ b/solution.py
@@ -174,8 +174,14 @@
     h_one = (normed1 * g_one.astype(f32) + s_one.astype(f32)).astype(jnp.bfloat16)
     bias_qkv = jnp.concatenate([full_bq.astype(f32), jnp.zeros((width,), f32), full_bv.astype(f32)])
     qkv = (jnp.dot(h_one, full_qkv, preferred_element_type=f32) + bias_qkv).astype(jnp.bfloat16)
-    grouped = lax.all_to_all(
-        qkv.reshape(rows, 3, width), "seq", split_axis=2, concat_axis=0, tiled=True
+    grouped = jnp.concatenate(
+        lax.all_to_all(
+            jnp.stack(jnp.split(qkv.reshape(rows, 3, width), lax.axis_size("seq"), axis=2)),
+            "seq",
+            0,
+            0,
+        ),
+        axis=0,
     )
     length = grouped.shape[0]
     local_width = grouped.shape[2]

time: 1250 us -> 1220 us (0.976)
  waiting for transfers between devices: 577 us -> 556 us
    all_to_all x1, waiting for transfers between devices: 101 us -> 75.9 us  [per_device(): lax.all_to_all(jnp.stack(jnp.split(qkv.reshape(rows, 3, width), lax.axis_...]
where the time goes in v1:
time: 1220 us; the launch traced here: 1210 us
  waiting for transfers between devices  556 us (46%)
  matrix products  283 us (23%)
  blocking collectives  238 us (20%)
  local copies, waits for them, and re-layouts  62.6 us (5%)
  other arithmetic  24.5 us (2%)
  starting transfers between devices  15.3 us (1%)
  between operations  14.8 us (1%)
  loops' own time  14 us (1%)
    reduce_scatter x1, waiting for transfers between devices, per_device(): lax.psum_scatter(g_w_back, ('seq', 'shard'), scatter_dimension=0, tiled=T...  189 us
    reduce_scatter x1, waiting for transfers between devices, per_device(): lax.psum_scatter(g_w_in, ('seq', 'shard'), scatter_dimension=0, tiled=True)  188 us
    all_to_all x1, blocking collectives, per_device(): lax.all_to_all(stacked, 'seq', split_axis=0, concat_axis=2, tiled=True)  97.2 us
    unnamed x2, blocking collectives  86.5 us
    all_to_all x1, waiting for transfers between devices, per_device(): lax.all_to_all(jnp.stack(jnp.split(qkv.reshape(rows, 3, width), lax.axis_...  75.9 us
    all_gather x1, blocking collectives, per_device(): lax.all_gather(bias_in, ('seq', 'shard'), axis=0, tiled=True)  54.7 us
    reduce_scatter x1, waiting for transfers between devices, per_device(): lax.psum_scatter(g_w_qkv, ('seq', 'shard'), scatter_dimension=0, tiled=True)  48.2 us
    dot_general x4, matrix products, one_block(): jnp.einsum('qgd,kgd->gqk', do_blk, values, preferred_element_type=jnp.flo...  42.1 us
  transfers between devices with their start and end apart: 11, of which 7 were waited for; matrix products, arithmetic and copies ran while one was open for 28% of the time, Pallas kernels for 0%

profile of v1, /device:TPU:13, one launch (start us, length us, event | category | flops | bytes accessed | tf_op | source)
XLA Modules:
  0.0 1208.5 jit_solution(5220360169140107189)
XLA Ops:
  16.1 40.8 %all-reduce.18 = (bf16[1024]{0:T(1024)(128)(2,1)S(1)}, bf16[1024]{0:T(1024)(128)(2,1)S(1)}, bf16[1024]{0:T(1024)(128)(2,1)S(1)}, bf16[1024]{0:T(1024)(128)(2,1)S...) all-reduce(bf16[1024]{0:T(1024)(128)(2,1)S(1)} %dynamic-update-slic, ...), channel_id=1, replica_groups=mesh['seq'=4,'shard'=8] {'seq','shard'}, use_global_device_ids=true, to_apply=%add.3 | all-reduce | flops 8192 | bytes 32768
  60.1 21.6 %all-gather.6.cloned.1.call-done = bf16[1024,3072]{1,0:T(8,128)(2,1)} async-done(((bf16[32,3072]{1,0:T(8,128)(2,1)}), bf16[1024,3072]{1,0:T(8,128)(2,1)}) %all-gather.6.cloned.1.call-update) | async-done | bytes 6291472 | tf_op jit(solution)/shard_map/all_gather | solution.py:143
  81.7 8.4 add_convert_fusion
  90.1 3.2 copy.71
  95.4 3.9 all-to-all-start
  99.9 75.9 %all-to-all-done = bf16[4,512,3,256]{1,3,2,0:T(8,128)(2,1)S(1)} async-done(((bf16[4,512,3,256]{1,3,2,0:T(8,128)(2,1)}), bf16[4,512,3,256]{1,3,2,0:T(8,128)(2,1)S(1)}, u32[]{:S(2)}, u32[]{:S(2)}) %all-to-all-start) | async-done | bytes 3145760 | tf_op jit(solution)/shard_map/all_to_all | solution.py:178
  175.7 2.9 copy.72
  184.5 50.8 %while.27 = (s32[]{:T(128)}, bf16[4,512,4,64]{1,3,2,0:T(8,128)(2,1)}, f32[4,4,512]{2,1,0:T(4,128)}, s32[4]{0:T(128)S(1)}, bf16[2048,4,64]{0,2,1:T(8,128)(2,1)S(1...) while((s32[]{:T(128)}, ...), condition=%wide.region_4.5_spmd, body=%wide.region_2.4_spmd.sunk | while | flops 1104280064 | bytes 43569372 | solution.py:64
  186.4 4.7 exponential_reduce_fusion.2
  191.1 5.5 fusion.127
  199.1 4.7 exponential_reduce_fusion.2
  203.8 5.5 fusion.127
  211.8 4.7 exponential_reduce_fusion.2
  216.5 5.5 fusion.127
  224.5 4.7 exponential_reduce_fusion.2
  229.2 5.5 fusion.127
  236.3 6.3 all-to-all-start.1
  242.7 54.7 %all-gather = bf16[32,1,128]{2,1,0:T(2,128)(2,1)S(1)} all-gather(bf16[1,1,128]{2,1,0:T(2,128)(2,1)S(1)} %bitcast.192), channel_id=1, replica_groups=mesh['seq'=4,'shard'=8] {'seq','shard'}, dimensions={0}, use_global_device_ids=true | all-gather | bytes 8448 | tf_op jit(solution)/shard_map/all_gather | solution.py:151
  298.5 4.2 fusion.86
  303.2 10.6 fusion.83
  313.8 15.4 %all-gather.12.cloned.1.call-done = bf16[4096,1024]{1,0:T(8,128)(2,1)} async-done(((bf16[128,1024]{1,0:T(8,128)(2,1)}), bf16[4096,1024]{1,0:T(8,128)(2,1)}) %all-gather.12.cloned.1.call-update) | async-done | bytes 8388624 | tf_op jit(solution)/shard_map/all_gather | solution.py:152
  329.2 15.0 %convert_reduce_fusion = (f32[4096]{0:T(1024)}, bf16[512,4096]{1,0:T(8,128)(2,1)}) fusion(f32[512,4096]{1,0:T(8,128)} %fusion.83, f32[4096]{0:T(1024)S(1)} %bitcast.189, bf16[4096,1024]{1,0:T(8,128)(2,1)} %all-gather.12.cloned.1.call-done, bf16[1,512,1024]{2,1,0:T(8,128)(2,1)} %param.33), kind=kOutput, calls=%fused_computation.52 | convolution fusion | flops 4341100544 | bytes 22052864 | tf_op jit(solution)/shard_map/dot_general | solution.py:117
  344.3 7.7 multiply_reduce_fusion.1
  352.0 3.3 fusion.84
  357.8 4.4 all-to-all-start.2
  362.2 2.4 copy.84
  364.6 4.5 fusion.79
  369.1 15.7 %all-to-all-done.2 = bf16[512,4,256]{2,0,1:T(8,128)(2,1)} async-done(((bf16[512,4,256]{2,0,1:T(8,128)(2,1)}), bf16[512,4,256]{2,0,1:T(8,128)(2,1)}, u32[]{:S(2)}, u32[]{:S(2)}) %all-to-all-start.2) | async-done | bytes 1048608 | tf_op jit(solution)/shard_map/all_to_all | solution.py:220
  388.5 156.1 %while.28 = (s32[]{:T(128)}, f32[2048,4,64]{0,2,1:T(8,128)}, f32[2048,4,64]{0,2,1:T(8,128)}, bf16[4,512,4,64]{1,3,2,0:T(8,128)(2,1)}, s32[4]{0:T(128)S(1)}, /*in...) while((s32[]{:T(128)}, f32[2048,4,64]{0,2,1:T(8,128)}, ...), condition=%wide.region_11.12_spmd.clone, body=%wide.region_9.11_spmd.clone.sunk | while | flops 2734291456 | bytes 138236336 | solution.py:100
  394.5 3.5 fusion.138
  398.0 7.2 fusion.140
  405.2 10.5 multiply_convert_fusion.5
  415.8 7.0 fusion.141
  422.8 4.0 fusion.139
  432.5 3.6 fusion.138
  436.1 7.6 fusion.140
  443.7 10.5 multiply_convert_fusion.5
  454.3 7.0 fusion.141
  461.2 4.8 fusion.139
  471.7 3.5 fusion.138
  475.2 7.6 fusion.140
  482.9 10.5 multiply_convert_fusion.5
  493.4 6.9 fusion.141
  500.3 4.8 fusion.139
  510.8 3.5 fusion.138
  514.4 7.6 fusion.140
  522.0 10.5 multiply_convert_fusion.5
  532.5 6.9 fusion.141
  539.4 4.8 fusion.139
  544.6 2.2 copy.79
  550.8 4.8 copy.80
  555.6 97.2 %all_to_all.55 = bf16[2048,3,256]{2,1,0:T(4,128)(2,1)S(1)} all-to-all(bf16[2048,3,256]{2,1,0:T(4,128)(2,1)} %copy.80), channel_id=1, replica_groups=mesh['seq'=4,'shard'=8] {'seq'}, dimensions={0} | all-to-all | bytes 6291456 | tf_op jit(solution)/shard_map/all_to_all | solution.py:232
  652.7 2.1 copy.81
  654.8 4.8 copy.82
  659.6 8.6 fusion.65
  669.5 16.2 %fusion.68 = f32[4096,1024]{1,0:T(8,128)} fusion(bf16[1,512,1024]{2,1,0:T(8,128)(2,1)S(1)} %copy-done.16, f32[512,4096]{1,0:T(8,128)} %fusion.83, f32[4096]{0:T(1024)S(1)} %bitcast.190), kind=kOutput, calls=%fused_computation.99 | convolution fusion | flops 4315938816 | bytes 26230784 | tf_op jit(solution)/shard_map/dot_general | solution.py:111
  687.4 11.5 fusion.82
  699.6 13.2 %fusion.63 = bf16[1,512,1024]{2,1,0:T(8,128)(2,1)} fusion(f32[512,1024]{1,0:T(8,128)S(1)} %copy-done.6, bf16[4096,1024]{1,0:T(8,128)(2,1)} %all-gather.12.cloned.1.call-done, f32[1024]{0:T(1024)S(1)} %convert_element_type.124, f32[512,4096]{1,0:T(8,128)} %fusion.83, f32[4096]{0:T(1024)S(1)} %bitcast.191), kind=kOutput, calls=%fused_computation.95 | convolution fusion | flops 4317511680 | bytes 19943424 | tf_op jit(solution)/shard_map/dot_general | solution.py:203
  713.3 8.8 fusion.56
  722.1 45.7 %all-reduce.17 = (f32[1024]{0:T(1024)S(1)}, f32[1024]{0:T(1024)S(1)}, f32[1024]{0:T(1024)S(1)}, f32[1024]{0:T(1024)S(1)}, f32[1024]{0:T(1024)S(1)}, /*index=5*/f...) all-reduce(f32[1024]{0:T(1024)S(1)} %get-tuple-element.184, ...), channel_id=2, replica_groups=mesh['seq'=4,'shard'=8] {'seq','shard'}, use_global_device_ids=true, to_apply=%region_15.16.clone | all-reduce | flops 12288 | bytes 98304
  773.1 3.6 fusion.55
  776.7 48.2 %reduce-scatter.5.cloned.1.call-done = f32[32,3072]{1,0:T(8,128)} async-done(((f32[1024,3072]{1,0:T(8,128)}), f32[32,3072]{1,0:T(8,128)}) %reduce-scatter.5.cloned.1.call-update) | async-done | bytes 393232 | tf_op jit(solution)/shard_map/reduce_scatter | solution.py:245
  824.9 189.0 %reduce-scatter.11.cloned.1.call-done = f32[128,1024]{1,0:T(8,128)} async-done(((f32[4096,1024]{1,0:T(8,128)}), f32[128,1024]{1,0:T(8,128)}) %reduce-scatter.11.cloned.1.call-update) | async-done | bytes 524304 | tf_op jit(solution)/shard_map/reduce_scatter | solution.py:254
  1013.9 187.5 %reduce-scatter.9.cloned.1.call-done = f32[32,4096]{1,0:T(8,128)} async-done(((f32[1024,4096]{1,0:T(8,128)}), f32[32,4096]{1,0:T(8,128)}) %reduce-scatter.9.cloned.1.call-update) | async-done | bytes 524304 | tf_op jit(solution)/shard_map/reduce_scatter | solution.py:252
  (254 shorter events, 62.2 us)
Async XLA Ops:
  7.2 74.5 %all-gather.6.cloned.1.call-start = ((), (), s32[]{:S(2)}) async-start(), calls=%async_computation.8 | async-start | bytes 6488064 | tf_op jit(solution)/shard_map/all_gather | solution.py:143
  7.9 289.6 %all-gather.8.cloned.1.call-start = ((), (), s32[]{:S(2)}) async-start(), calls=%async_computation.9 | async-start | bytes 2162688 | tf_op jit(solution)/shard_map/all_gather | solution.py:146
  8.7 294.5 %all-gather.10.cloned.1.call-start = ((), (), s32[]{:S(2)}) async-start(), calls=%async_computation.10 | async-start | bytes 8650752 | tf_op jit(solution)/shard_map/all_gather | solution.py:150
  56.9 24.8 %copy-start.25 = (f32[1024]{0:T(1024)}, f32[1024]{0:T(1024)S(1)}, u32[]{:S(2)}) copy-start(f32[1024]{0:T(1024)S(1)} %convert_element_type.112) | copy-start | bytes 12292
  56.9 24.8 %copy-start.38 = (f32[1024]{0:T(1024)}, f32[1024]{0:T(1024)S(1)}, u32[]{:S(2)}) copy-start(f32[1024]{0:T(1024)S(1)} %convert_element_type.113) | copy-start | bytes 12292
  58.4 23.3 %copy-start.21 = (f32[512]{0:T(512)}, f32[512]{0:T(512)S(1)}, u32[]{:S(2)}) copy-start(f32[512]{0:T(512)S(1)} %broadcast_multiply_fusion.5) | copy-start | bytes 6148
  60.1 21.6 %copy-start.34 = (f32[512]{0:T(512)}, f32[512]{0:T(512)S(1)}, u32[]{:S(2)}) copy-start(f32[512]{0:T(512)S(1)} %add_rsqrt_fusion.1) | copy-start | bytes 6148
  95.4 80.3 %all-to-all-start = ((bf16[4,512,3,256]{1,3,2,0:T(8,128)(2,1)}), bf16[4,512,3,256]{1,3,2,0:T(8,128)(2,1)S(1)}, u32[]{:S(2)}, u32[]{:S(2)}) async-start(bf16[4,512,3,256]{1,3,2,0:T(8,128)(2,1)} %pad_maximum_fusion), calls=%async_computation | async-start | bytes 6291456 | tf_op jit(solution)/shard_map/all_to_all | solution.py:178
  99.3 229.9 %all-gather.12.cloned.1.call-start = ((), (), s32[]{:S(2)}) async-start(), calls=%async_computation.11 | async-start | bytes 8650752 | tf_op jit(solution)/shard_map/all_gather | solution.py:152
  184.5 58.2 %copy-start.43 = (bf16[128]{0:T(256)(128)(2,1)S(1)}, bf16[128]{0:T(256)(128)(2,1)}, u32[]{:S(2)}) copy-start(bf16[128]{0:T(256)(128)(2,1)} %param.30) | copy-start | bytes 772
  186.4 4.7 copy-start.17
  199.1 4.7 copy-start.17
  211.8 4.7 copy-start.17
  224.5 4.7 copy-start.17
  236.3 61.2 %all-to-all-start.1 = ((bf16[4,512,256]{1,2,0:T(8,128)(2,1)}), bf16[4,512,256]{1,2,0:T(8,128)(2,1)S(1)}, u32[]{:S(2)}, u32[]{:S(2)}) async-start(bf16[4,512,256]{1,2,0:T(8,128)(2,1)} %bitcast.14), calls=%async_computation.1 | async-start | bytes 2097152 | tf_op jit(solution)/shard_map/all_to_all | solution.py:193
  242.6 109.3 %copy-start.27 = (f32[1024]{0:T(1024)}, f32[1024]{0:T(1024)S(1)}, u32[]{:S(2)}) copy-start(f32[1024]{0:T(1024)S(1)} %convert_element_type.119) | copy-start | bytes 12292
  242.7 60.5 %copy-start.40 = (f32[1024]{0:T(1024)}, f32[1024]{0:T(1024)S(1)}, u32[]{:S(2)}) copy-start(f32[1024]{0:T(1024)S(1)} %convert_element_type.120) | copy-start | bytes 12292
  297.4 31.8 %copy-start.30 = (f32[32,1,128]{2,1,0:T(1,128)}, f32[32,1,128]{2,1,0:T(1,128)S(1)}, u32[]{:S(2)}) copy-start(f32[32,1,128]{2,1,0:T(1,128)S(1)} %convert_element_type.137) | copy-start | bytes 49156
  302.8 41.5 %copy-start.5 = (f32[512,1024]{1,0:T(8,128)}, f32[512,1024]{1,0:T(8,128)S(1)}, u32[]{:S(2)}) copy-start(f32[512,1024]{1,0:T(8,128)S(1)} %get-tuple-element.258) | copy-start | bytes 6291460
  302.8 49.2 %copy-start.19 = (f32[512]{0:T(512)}, f32[512]{0:T(512)S(1)}, u32[]{:S(2)}) copy-start(f32[512]{0:T(512)S(1)} %broadcast_multiply_fusion.4) | copy-start | bytes 6148
  303.1 48.8 %copy-start.32 = (f32[512]{0:T(512)}, f32[512]{0:T(512)S(1)}, u32[]{:S(2)}) copy-start(f32[512]{0:T(512)S(1)} %add_rsqrt_fusion) | copy-start | bytes 6148
  329.2 15.0 %copy-start.44 = (bf16[1024,4096]{1,0:T(8,128)(2,1)S(1)}, bf16[1024,4096]{1,0:T(8,128)(2,1)}, u32[]{:S(2)}) copy-start(bf16[1024,4096]{1,0:T(8,128)(2,1)} %all-gather.10.cloned.1.call-done) | copy-start | bytes 25165828
  344.3 7.7 copy-start.15
  352.0 3.4 copy-start.14
  355.4 9.2 copy-start.3
  357.8 27.0 %all-to-all-start.2 = ((bf16[512,4,256]{2,0,1:T(8,128)(2,1)}), bf16[512,4,256]{2,0,1:T(8,128)(2,1)}, u32[]{:S(2)}, u32[]{:S(2)}) async-start(bf16[512,4,256]{2,0,1:T(8,128)(2,1)} %bitcast.183), calls=%async_computation.2 | async-start | bytes 2097152 | tf_op jit(solution)/shard_map/all_to_all | solution.py:220
  362.2 414.5 %reduce-scatter.7.cloned.1.call-start = ((), (), s32[]{:S(2)}) async-start(), calls=%async_computation.13 | async-start | bytes 4325376 | tf_op jit(solution)/shard_map/reduce_scatter | solution.py:248
  369.1 455.9 %reduce-scatter.5.cloned.1.call-start = ((), (), s32[]{:S(2)}) async-start(), calls=%async_computation.12 | async-start | bytes 12976128 | tf_op jit(solution)/shard_map/reduce_scatter | solution.py:245
  388.7 5.0 copy-start.11
  392.7 5.3 copy-start.18
  394.4 3.6 copy-start.2
  415.8 7.0 copy-start
  422.8 4.0 copy-start.12
  426.8 5.0 copy-start.11
  430.8 5.3 copy-start.18
  432.5 3.6 copy-start.2
  454.3 7.0 copy-start
  461.2 4.8 copy-start.12
  466.0 5.0 copy-start.11
  469.9 5.3 copy-start.18
  471.7 3.6 copy-start.2
  493.4 6.9 copy-start
  500.3 4.8 copy-start.12
  505.1 5.0 copy-start.11
  509.1 5.3 copy-start.18
  510.8 3.6 copy-start.2
  532.5 6.9 copy-start
  539.4 4.8 copy-start.12
  544.6 3.8 copy-start.1
  548.4 2.0 copy-start.13
  654.8 4.8 copy-start.7
  654.8 4.8 copy-start.22
  654.8 4.8 copy-start.26
  654.8 4.8 copy-start.35
  654.8 4.8 copy-start.39
  668.3 345.7 %reduce-scatter.11.cloned.1.call-start = ((), (), s32[]{:S(2)}) async-start(), calls=%async_computation.15 | async-start | bytes 17301504 | tf_op jit(solution)/shard_map/reduce_scatter | solution.py:254
  685.8 515.7 %reduce-scatter.9.cloned.1.call-start = ((), (), s32[]{:S(2)}) async-start(), calls=%async_computation.14 | async-start | bytes 17301504 | tf_op jit(solution)/shard_map/reduce_scatter | solution.py:252
  699.6 13.2 %copy-start.10 = (bf16[512,3,4,256]{0,3,2,1:T(8,128)(2,1)S(1)}, bf16[512,3,4,256]{0,3,2,1:T(8,128)(2,1)}, u32[]{:S(2)}) copy-start(bf16[512,3,4,256]{0,3,2,1:T(8,128)(2,1)} %copy.82) | copy-start | bytes 9437188
  713.2 8.8 copy-start.23
  713.2 8.8 copy-start.24
  713.2 8.8 copy-start.29
  713.2 8.8 copy-start.36
  713.2 8.8 copy-start.37
  713.3 59.8 %copy-start.4 = (f32[512,1024]{1,0:T(8,128)S(1)}, f32[512,1024]{1,0:T(8,128)}, u32[]{:S(2)}) copy-start(f32[512,1024]{1,0:T(8,128)} %copy-done.3) | copy-start | bytes 6291460
  (10 other events, 13.7 us)
Sparse Core Ops, SparseCore 0:
  10.8 70.8 all-gather.5
  84.6 82.3 all-gather.7
  169.8 75.5 all-gather.9
  248.1 81.0 all-gather.11
  369.2 115.2 reduce-scatter.6
  668.4 156.4 reduce-scatter.4
  827.8 186.1 reduce-scatter.10
  1016.8 184.6 reduce-scatter.8
